TPU v7x, 8 devices: a whole 2x2x1 slice. The times are simulated.
8 devices in a mesh: hp: 1 (over z), cp: 8 (over y, x, core).
Axes of the slice: x: 2, y: 2, z: 1, core: 2. Of those that a mesh axis runs over, the one named last changes fastest.
Arguments:
- q: bfloat16 [3072, 32, 128], P('cp', 'hp')
- k: bfloat16 [3072, 32, 128], P('cp', 'hp')
- v: bfloat16 [3072, 32, 128], P('cp', 'hp')
- u_bias: float32 [32, 128], P('hp')
- v_bias: float32 [32, 128], P('hp')
- rel_table: bfloat16 [3072, 4096], P('cp')
- w_rel: bfloat16 [4096, 32, 128], P(None, 'hp')
- d_out: bfloat16 [3072, 32, 128], P('cp', 'hp')
Outputs:
- output 1: bfloat16 [3072, 32, 128], P('cp', 'hp')
- output 2: bfloat16 [3072, 32, 128], P('cp', 'hp')
- output 3: bfloat16 [3072, 32, 128], P('cp', 'hp')
- output 4: bfloat16 [3072, 32, 128], P('cp', 'hp')
- output 5: float32 [32, 128], P('hp')
- output 6: float32 [32, 128], P('hp')
- output 7: float32 [4096, 32, 128], P(None, 'hp')
All inputs are finite; a program needn't handle non-finite values.
Results may differ from a plain program's by a relative error of at most 0.016366.
Values are sent between devices in bfloat16 or wider.
A program may use at most 1 GiB of HBM per device.

v0:
```python
import jax
import jax.numpy as jnp
from jax import lax
from jax.sharding import PartitionSpec as P


def skew_scores(by_offset):
    lead_dims = by_offset.shape[:-2]
    block_len = by_offset.shape[-2]
    flat_view = by_offset.reshape(lead_dims + (2 * block_len * block_len,))
    kept_view = flat_view[..., block_len - 1:block_len - 1 + block_len * (2 * block_len - 1)]
    return kept_view.reshape(lead_dims + (block_len, 2 * block_len - 1))[..., :block_len]


def unskew_scores(by_key):
    lead_dims = by_key.shape[:-2]
    block_len = by_key.shape[-1]
    pad_lead = [(0, 0)] * len(lead_dims)
    widened = jnp.pad(by_key, pad_lead + [(0, 0), (0, block_len - 1)])
    flat_view = widened.reshape(lead_dims + (block_len * (2 * block_len - 1),))
    flat_view = jnp.pad(flat_view, pad_lead + [(block_len - 1, 1)])
    return flat_view.reshape(lead_dims + (block_len, 2 * block_len))


def solution(mesh):
    n_dev = mesh.shape['cp']
    shift_pairs = [(src_dev, (src_dev + 1) % n_dev) for src_dev in range(n_dev)]
    last_step = n_dev - 1
    seq_spec = P('cp', 'hp', None)
    head_spec = P('hp', None)
    weight_spec = P(None, 'hp', None)

    def local_fn(q, k, v, u_bias, v_bias, rel_table, w_rel, d_out):
        block_len, num_heads, head_dim = q.shape
        inv_sqrt = head_dim ** -0.5
        my_block = lax.axis_index('cp')
        rel_mine = jnp.einsum('uo,ojf->ujf', rel_table, w_rel, preferred_element_type=jnp.float32).astype(jnp.bfloat16)
        rel_flipped = lax.all_gather(rel_mine[::-1], 'cp')
        q_wide = q.astype(jnp.float32)
        q_u = (q_wide + u_bias).astype(jnp.bfloat16)
        q_v = (q_wide + v_bias).astype(jnp.bfloat16)
        row_ids = jnp.arange(block_len)
        above_diag = row_ids[None, :] > row_ids[:, None]

        def rel_window(distance):
            near_blk = lax.dynamic_index_in_dim(rel_flipped, distance, 0, keepdims=False)
            far_blk = lax.dynamic_index_in_dim(rel_flipped, jnp.maximum(distance - 1, 0), 0, keepdims=False)
            return jnp.concatenate([near_blk, far_blk], axis=0)

        def block_scores(k_blk, window, distance):
            content = jnp.einsum('qhd,khd->hqk', q_u, k_blk, preferred_element_type=jnp.float32)
            by_offset = jnp.einsum('qhd,shd->hqs', q_v, window, preferred_element_type=jnp.float32)
            score_ij = (content + skew_scores(by_offset)) * inv_sqrt
            return jnp.where(above_diag & (distance == 0), -jnp.inf, score_ij)

        def attend(distance, k_blk, v_blk, run_stats):
            run_max, run_sum, out_acc = run_stats
            score_ij = block_scores(k_blk, rel_window(distance), distance)
            new_max = jnp.maximum(run_max, score_ij.max(axis=-1))
            prob_ij = jnp.exp(score_ij - new_max[..., None])
            rescale = jnp.exp(run_max - new_max)
            run_sum = rescale * run_sum + prob_ij.sum(axis=-1)
            out_acc = out_acc * rescale.T[:, :, None] + jnp.einsum('hqk,khd->qhd', prob_ij.astype(jnp.bfloat16), v_blk, preferred_element_type=jnp.float32)
            return new_max, run_sum, out_acc

        def fwd_step(step_idx, carry):
            k_blk, v_blk, run_stats = carry
            run_stats = lax.cond(step_idx <= my_block, lambda stats_in: attend(step_idx, k_blk, v_blk, stats_in), lambda stats_in: stats_in, run_stats)
            k_blk = lax.ppermute(k_blk, 'cp', shift_pairs)
            v_blk = lax.ppermute(v_blk, 'cp', shift_pairs)
            return k_blk, v_blk, run_stats

        run_stats = (
            jnp.full((num_heads, block_len), -jnp.inf, jnp.float32),
            jnp.zeros((num_heads, block_len), jnp.float32),
            jnp.zeros((block_len, num_heads, head_dim), jnp.float32),
        )
        k_blk, v_blk, run_stats = lax.fori_loop(0, last_step, fwd_step, (k, v, run_stats))
        run_stats = lax.cond(last_step <= my_block, lambda stats_in: attend(last_step, k_blk, v_blk, stats_in), lambda stats_in: stats_in, run_stats)
        run_max, run_sum, out_acc = run_stats
        out_full = out_acc / run_sum.T[:, :, None]
        log_norm = run_max + jnp.log(run_sum)
        row_delta = jnp.sum(d_out.astype(jnp.float32) * out_full, axis=-1).T

        def grad_block(distance, k_blk, v_blk, grad_state):
            dk_acc, dv_acc, grad_qu, grad_qv, grad_rel = grad_state
            window = rel_window(distance)
            score_ij = block_scores(k_blk, window, distance)
            prob_ij = jnp.exp(score_ij - log_norm[..., None])
            d_prob = jnp.einsum('qhd,khd->hqk', d_out, v_blk, preferred_element_type=jnp.float32)
            d_score = (prob_ij * (d_prob - row_delta[..., None]) * inv_sqrt).astype(jnp.bfloat16)
            dv_acc = dv_acc + jnp.einsum('hqk,qhd->khd', prob_ij.astype(jnp.bfloat16), d_out, preferred_element_type=jnp.float32)
            dk_acc = dk_acc + jnp.einsum('hqk,qhd->khd', d_score, q_u, preferred_element_type=jnp.float32)
            grad_qu = grad_qu + jnp.einsum('hqk,khd->qhd', d_score, k_blk, preferred_element_type=jnp.float32)
            d_wide = unskew_scores(d_score)
            grad_qv = grad_qv + jnp.einsum('hqs,shd->qhd', d_wide, window, preferred_element_type=jnp.float32)
            d_window = jnp.einsum('hqs,qhd->shd', d_wide, q_v, preferred_element_type=jnp.float32)
            near_sum = lax.dynamic_index_in_dim(grad_rel, distance, 0, keepdims=False) + d_window[:block_len]
            grad_rel = lax.dynamic_update_index_in_dim(grad_rel, near_sum, distance, 0)
            far_idx = jnp.maximum(distance - 1, 0)
            far_sum = lax.dynamic_index_in_dim(grad_rel, far_idx, 0, keepdims=False) + d_window[block_len:]
            grad_rel = lax.dynamic_update_index_in_dim(grad_rel, far_sum, far_idx, 0)
            return dk_acc, dv_acc, grad_qu, grad_qv, grad_rel

        def bwd_step(step_idx, carry):
            k_blk, v_blk, grad_state = carry
            grad_state = lax.cond(step_idx <= my_block, lambda grads_in: grad_block(step_idx, k_blk, v_blk, grads_in), lambda grads_in: grads_in, grad_state)
            dk_acc, dv_acc, grad_qu, grad_qv, grad_rel = grad_state
            k_blk = lax.ppermute(k_blk, 'cp', shift_pairs)
            v_blk = lax.ppermute(v_blk, 'cp', shift_pairs)
            dk_acc = lax.ppermute(dk_acc, 'cp', shift_pairs)
            dv_acc = lax.ppermute(dv_acc, 'cp', shift_pairs)
            return k_blk, v_blk, (dk_acc, dv_acc, grad_qu, grad_qv, grad_rel)

        blk_zeros = jnp.zeros((block_len, num_heads, head_dim), jnp.float32)
        grad_state = (blk_zeros, blk_zeros, blk_zeros, blk_zeros, jnp.zeros((n_dev, block_len, num_heads, head_dim), jnp.float32))
        k_blk, v_blk, grad_state = lax.fori_loop(0, last_step, bwd_step, (k, v, grad_state))
        grad_state = lax.cond(last_step <= my_block, lambda grads_in: grad_block(last_step, k_blk, v_blk, grads_in), lambda grads_in: grads_in, grad_state)
        dk_acc, dv_acc, grad_qu, grad_qv, grad_rel = grad_state
        dk_acc = lax.ppermute(dk_acc, 'cp', shift_pairs)
        dv_acc = lax.ppermute(dv_acc, 'cp', shift_pairs)
        rel_grad_mine = lax.psum_scatter(grad_rel, 'cp', scatter_dimension=0, tiled=False)
        d_rel = rel_grad_mine[::-1].astype(jnp.bfloat16)
        d_w_rel = lax.psum(jnp.einsum('uo,ujf->ojf', rel_table, d_rel, preferred_element_type=jnp.float32), 'cp')
        d_u_bias = lax.psum(grad_qu.sum(axis=0), 'cp')
        d_v_bias = lax.psum(grad_qv.sum(axis=0), 'cp')
        return (
            out_full.astype(jnp.bfloat16),
            (grad_qu + grad_qv).astype(jnp.bfloat16),
            dk_acc.astype(jnp.bfloat16),
            dv_acc.astype(jnp.bfloat16),
            d_u_bias,
            d_v_bias,
            d_w_rel,
        )

    return jax.shard_map(
        local_fn,
        mesh=mesh,
        in_specs=(seq_spec, seq_spec, seq_spec, head_spec, head_spec, P('cp', None), weight_spec, seq_spec),
        out_specs=(seq_spec, seq_spec, seq_spec, seq_spec, head_spec, head_spec, weight_spec),
        check_vma=False,
    )
```

profile of v0, /device:TPU:0, one launch (start us, length us, event | category | flops | bytes accessed | tf_op | source)
XLA Modules:
  0.0 7901.8 jit_solution(332383539614809374)
XLA Ops:
  29.5 45.3 rev.6
  98.9 98.6 %all-gather.3.cloned.1.call-done = bf16[3072,32,128]{2,0,1:T(8,128)(2,1)} async-done(((bf16[384,32,128]{2,0,1:T(8,128)(2,1)}), bf16[3072,32,128]{2,0,1:T(8,128)(2,1)}) %all-gather.3.cloned.1.call-update) | async-done | bytes 25165840 | tf_op jit(solution)/shard_map/all_gather | solution.py:38
  224.1 1608.5 %while.48 = (s32[]{:T(128)}, bf16[384,32,128]{2,0,1:T(8,128)(2,1)}, bf16[384,32,128]{2,0,1:T(8,128)(2,1)}, f32[32,384]{1,0:T(8,128)S(1)}, f32[32,384]{1,0:T(8,12...) while((s32[]{:T(128)}, bf16[384,32,128]{2,0,1:T(8,128)(2,1)}, ...), condition=%wide.region_5.6_spmd.clone, body=%wide.region_0.5_spmd.clone.sunk | while | flops 4885647360 | bytes 500269472 | solution.py:78
  251.3 243.0 %conditional.10 = ((f32[32,384]{1,0:T(8,128)S(1)}, f32[32,384]{1,0:T(8,128)S(1)}, f32[384,32,128]{2,0,1:T(8,128)})) conditional(s32[]{:T(128)} %convert_element_type.120, (f32[32,384]{1,0:T(8,128)S(1)}, f32[32,384]{1,0:T(8,128)S(1)}, f32[384,32,128]{2,0,1:T(8,128)}) %tuple.144, (s32[]{:T(128)}, s32[384,384]{0,1:T(8,128)}, ...), branch_computations={%region_1.0_spmd, %region_2.4_spmd} | conditional | flops 4885647360 | bytes 461340768 | solution.py:68
  276.1 37.9 copy.138
  314.1 30.2 slice.44
  344.3 74.9 reshape.50
  504.1 31.7 collective-permute-done
  535.8 33.7 collective-permute-done.1
  573.4 177.6 %collective-permute-start = (bf16[384,32,128]{2,0,1:T(8,128)(2,1)}, bf16[384,32,128]{2,0,1:T(8,128)(2,1)}, u32[]{:S(2)}, u32[]{:S(2)}) collective-permute-start(bf16[384,32,128]{2,0,1:T(8,128)(2,1)} %copy.199), channel_id=1, source_target_pairs={{0,1},{1,2},{2,3},{3,4},{4,5},{5,6},{6,7},{7,0}} | collective-permute-start | bytes 9437192 | tf_op jit(solution)/shard_map/while/body/eval_jaxpr/ppermute | solution.py:69
  756.6 32.0 collective-permute-done
  788.5 33.7 collective-permute-done.1
  830.0 177.3 %collective-permute-start.1 = (bf16[384,32,128]{2,0,1:T(8,128)(2,1)}, bf16[384,32,128]{2,0,1:T(8,128)(2,1)}, u32[]{:S(2)}, u32[]{:S(2)}) collective-permute-start(bf16[384,32,128]{2,0,1:T(8,128)(2,1)} %copy.200), channel_id=1, source_target_pairs={{0,1},{1,2},{2,3},{3,4},{4,5},{5,6},{6,7},{7,0}} | collective-permute-start | bytes 9437192 | tf_op jit(solution)/shard_map/while/body/eval_jaxpr/ppermute | solution.py:70
  1009.0 32.0 collective-permute-done
  1041.0 33.7 collective-permute-done.1
  1084.2 209.3 %collective-permute-done = bf16[384,32,128]{2,0,1:T(8,128)(2,1)} collective-permute-done((bf16[384,32,128]{2,0,1:T(8,128)(2,1)}, bf16[384,32,128]{2,0,1:T(8,128)(2,1)}, u32[]{:S(2)}, u32[]{:S(2)}) %collective-permute-start) | collective-permute-done | bytes 3145760 | tf_op jit(solution)/shard_map/while/body/eval_jaxpr/ppermute | solution.py:69
  1293.5 33.7 collective-permute-done.1
  1336.7 209.3 %collective-permute-done = bf16[384,32,128]{2,0,1:T(8,128)(2,1)} collective-permute-done((bf16[384,32,128]{2,0,1:T(8,128)(2,1)}, bf16[384,32,128]{2,0,1:T(8,128)(2,1)}, u32[]{:S(2)}, u32[]{:S(2)}) %collective-permute-start) | collective-permute-done | bytes 3145760 | tf_op jit(solution)/shard_map/while/body/eval_jaxpr/ppermute | solution.py:69
  1546.0 33.7 collective-permute-done.1
  1589.2 209.3 %collective-permute-done = bf16[384,32,128]{2,0,1:T(8,128)(2,1)} collective-permute-done((bf16[384,32,128]{2,0,1:T(8,128)(2,1)}, bf16[384,32,128]{2,0,1:T(8,128)(2,1)}, u32[]{:S(2)}, u32[]{:S(2)}) %collective-permute-start) | collective-permute-done | bytes 3145760 | tf_op jit(solution)/shard_map/while/body/eval_jaxpr/ppermute | solution.py:69
  1798.5 33.7 collective-permute-done.1
  1884.8 4410.7 %while.49 = (s32[]{:T(128)}, bf16[384,32,128]{2,0,1:T(8,128)(2,1)}, bf16[384,32,128]{2,0,1:T(8,128)(2,1)}, f32[384,32,128]{2,0,1:T(8,128)}, f32[384,32,128]{2,0,...) while((s32[]{:T(128)}, bf16[384,32,128]{2,0,1:T(8,128)(2,1)}, ...), condition=%wide.region_14.15_spmd.clone, body=%wide.region_11.14_spmd.clone.sunk | while | flops 13364920320 | bytes 943030912 | solution.py:117
  1894.6 358.3 %conditional.11 = ((f32[384,32,128]{2,0,1:T(8,128)}, f32[384,32,128]{2,0,1:T(8,128)}, f32[384,32,128]{2,0,1:T(8,128)}, f32[384,32,128]{0,2,1:T(8,128)}, f32[8,384,32,128]{3,1,2,0:T(8,128)})) conditional(s32[]{:T(128)} %convert_element_type.121, (f32[384,32,128]{2,0,1:T(8,128)}, f32[384,32,128]{2,0,1:T(8,128)}, f32[384,32,128]{2,0,1:T(8,128)}, ...), branch_computations={%region_12.12_spmd, %region_13.13_spmd} | conditional | flops 13364920320 | bytes 828604608 | solution.py:107
  1918.4 37.9 copy.139
  1956.3 30.2 slice.46
  1986.5 75.0 reshape.54
  2133.4 44.6 reshape.55
  2253.0 478.3 %collective-permute-done.4 = f32[384,32,128]{2,0,1:T(8,128)} collective-permute-done((f32[384,32,128]{2,0,1:T(8,128)}, f32[384,32,128]{2,0,1:T(8,128)}, u32[]{:S(2)}, u32[]{:S(2)}) %collective-permute-start.4) | collective-permute-done | bytes 6291488 | tf_op jit(solution)/shard_map/while/body/eval_jaxpr/ppermute | solution.py:111
  2737.5 61.3 collective-permute-done.5
  2804.8 27.6 collective-permute-done.2
  2832.5 33.7 collective-permute-done.3
  2878.0 190.1 %collective-permute-start.2 = (bf16[384,32,128]{2,0,1:T(8,128)(2,1)}, bf16[384,32,128]{2,0,1:T(8,128)(2,1)}, u32[]{:S(2)}, u32[]{:S(2)}) collective-permute-start(bf16[384,32,128]{2,0,1:T(8,128)(2,1)} %copy.225), channel_id=1, source_target_pairs={{0,1},{1,2},{2,3},{3,4},{4,5},{5,6},{6,7},{7,0}} | collective-permute-start | bytes 9437192 | tf_op jit(solution)/shard_map/while/body/eval_jaxpr/ppermute | solution.py:109
  3071.5 230.5 %collective-permute-done.4 = f32[384,32,128]{2,0,1:T(8,128)} collective-permute-done((f32[384,32,128]{2,0,1:T(8,128)}, f32[384,32,128]{2,0,1:T(8,128)}, u32[]{:S(2)}, u32[]{:S(2)}) %collective-permute-start.4) | collective-permute-done | bytes 6291488 | tf_op jit(solution)/shard_map/while/body/eval_jaxpr/ppermute | solution.py:111
  3308.2 61.3 collective-permute-done.5
  3375.5 27.6 collective-permute-done.2
  3403.2 33.7 collective-permute-done.3
  3446.6 127.3 %collective-permute-start.5 = (f32[384,32,128]{2,0,1:T(8,128)}, f32[384,32,128]{2,0,1:T(8,128)}, u32[]{:S(2)}, u32[]{:S(2)}) collective-permute-start(f32[384,32,128]{2,0,1:T(8,128)} %get-tuple-element.1177), channel_id=1, source_target_pairs={{0,1},{1,2},{2,3},{3,4},{4,5},{5,6},{6,7},{7,0}} | collective-permute-start | bytes 18874376 | tf_op jit(solution)/shard_map/while/body/eval_jaxpr/ppermute | solution.py:112
  3573.9 98.6 %collective-permute-start.2 = (bf16[384,32,128]{2,0,1:T(8,128)(2,1)}, bf16[384,32,128]{2,0,1:T(8,128)(2,1)}, u32[]{:S(2)}, u32[]{:S(2)}) collective-permute-start(bf16[384,32,128]{2,0,1:T(8,128)(2,1)} %copy.225), channel_id=1, source_target_pairs={{0,1},{1,2},{2,3},{3,4},{4,5},{5,6},{6,7},{7,0}} | collective-permute-start | bytes 9437192 | tf_op jit(solution)/shard_map/while/body/eval_jaxpr/ppermute | solution.py:109
  3675.9 197.0 %collective-permute-done.4 = f32[384,32,128]{2,0,1:T(8,128)} collective-permute-done((f32[384,32,128]{2,0,1:T(8,128)}, f32[384,32,128]{2,0,1:T(8,128)}, u32[]{:S(2)}, u32[]{:S(2)}) %collective-permute-start.4) | collective-permute-done | bytes 6291488 | tf_op jit(solution)/shard_map/while/body/eval_jaxpr/ppermute | solution.py:111
  3879.1 61.3 collective-permute-done.5
  3946.5 27.6 collective-permute-done.2
  3974.1 33.7 collective-permute-done.3
  4017.4 229.5 %collective-permute-start.2 = (bf16[384,32,128]{2,0,1:T(8,128)(2,1)}, bf16[384,32,128]{2,0,1:T(8,128)(2,1)}, u32[]{:S(2)}, u32[]{:S(2)}) collective-permute-start(bf16[384,32,128]{2,0,1:T(8,128)(2,1)} %copy.225), channel_id=1, source_target_pairs={{0,1},{1,2},{2,3},{3,4},{4,5},{5,6},{6,7},{7,0}} | collective-permute-start | bytes 9437192 | tf_op jit(solution)/shard_map/while/body/eval_jaxpr/ppermute | solution.py:109
  4250.2 193.7 %collective-permute-done.4 = f32[384,32,128]{2,0,1:T(8,128)} collective-permute-done((f32[384,32,128]{2,0,1:T(8,128)}, f32[384,32,128]{2,0,1:T(8,128)}, u32[]{:S(2)}, u32[]{:S(2)}) %collective-permute-start.4) | collective-permute-done | bytes 6291488 | tf_op jit(solution)/shard_map/while/body/eval_jaxpr/ppermute | solution.py:111
  4450.1 61.3 collective-permute-done.5
  4545.1 33.7 collective-permute-done.3
  4588.4 236.2 %collective-permute-start.3 = (bf16[384,32,128]{2,0,1:T(8,128)(2,1)}, bf16[384,32,128]{2,0,1:T(8,128)(2,1)}, u32[]{:S(2)}, u32[]{:S(2)}) collective-permute-start(bf16[384,32,128]{2,0,1:T(8,128)(2,1)} %copy.226), channel_id=1, source_target_pairs={{0,1},{1,2},{2,3},{3,4},{4,5},{5,6},{6,7},{7,0}} | collective-permute-start | bytes 9437192 | tf_op jit(solution)/shard_map/while/body/eval_jaxpr/ppermute | solution.py:110
  4824.6 190.5 %collective-permute-done.4 = f32[384,32,128]{2,0,1:T(8,128)} collective-permute-done((f32[384,32,128]{2,0,1:T(8,128)}, f32[384,32,128]{2,0,1:T(8,128)}, u32[]{:S(2)}, u32[]{:S(2)}) %collective-permute-start.4) | collective-permute-done | bytes 6291488 | tf_op jit(solution)/shard_map/while/body/eval_jaxpr/ppermute | solution.py:111
  5021.3 61.3 collective-permute-done.5
  5088.6 27.6 collective-permute-done.2
  5116.3 33.7 collective-permute-done.3
  5159.6 426.2 %collective-permute-done.4 = f32[384,32,128]{2,0,1:T(8,128)} collective-permute-done((f32[384,32,128]{2,0,1:T(8,128)}, f32[384,32,128]{2,0,1:T(8,128)}, u32[]{:S(2)}, u32[]{:S(2)}) %collective-permute-start.4) | collective-permute-done | bytes 6291488 | tf_op jit(solution)/shard_map/while/body/eval_jaxpr/ppermute | solution.py:111
  5592.0 61.3 collective-permute-done.5
  5659.3 27.6 collective-permute-done.2
  5687.0 33.7 collective-permute-done.3
  5730.3 426.5 %collective-permute-done.4 = f32[384,32,128]{2,0,1:T(8,128)} collective-permute-done((f32[384,32,128]{2,0,1:T(8,128)}, f32[384,32,128]{2,0,1:T(8,128)}, u32[]{:S(2)}, u32[]{:S(2)}) %collective-permute-start.4) | collective-permute-done | bytes 6291488 | tf_op jit(solution)/shard_map/while/body/eval_jaxpr/ppermute | solution.py:111
  6162.9 61.3 collective-permute-done.5
  6257.9 33.7 collective-permute-done.3
  6312.0 616.6 %reduce-scatter.2.cloned.1.call-done = f32[1,384,32,128]{3,1,2,0:T(8,128)} async-done(((f32[8,384,32,128]{3,1,2,0:T(8,128)}), f32[1,384,32,128]{3,1,2,0:T(8,128)}) %reduce-scatter.2.cloned.1.call-update) | async-done | bytes 6291472 | tf_op jit(solution)/shard_map/reduce_scatter | solution.py:122
  6928.7 47.7 rev.7
  6976.4 28.8 convolution_bitcast_fusion.6
  7036.4 199.8 %all-reduce.4 = (f32[32,128]{1,0:T(8,128)}, f32[32,128]{1,0:T(8,128)}) all-reduce(f32[32,128]{1,0:T(8,128)S(1)} %reduce_sum.46, f32[32,128]{1,0:T(8,128)S(1)} %reduce_sum.47), channel_id=1, replica_groups=mesh['hp'=1,'cp'=8] {'cp'}, use_global_device_ids=true, to_apply=%region_18.19 | all-reduce | flops 8192 | bytes 65536 | tf_op jit(solution)/shard_map/psum | solution.py:125
  7246.3 574.6 %all-reduce.7.cloned.1.call-done = f32[4096,32,128]{0,2,1:T(8,128)} async-done(((f32[4096,32,128]{0,2,1:T(8,128)}), f32[4096,32,128]{0,2,1:T(8,128)}) %all-reduce.7.cloned.1.call-update) | async-done | bytes 67108880 | tf_op jit(solution)/shard_map/psum | solution.py:124
  7820.9 65.9 copy.121
  (207 shorter events, 765.3 us)
Async XLA Ops:
  7.2 1.9 copy-start
  7.2 190.3 %all-gather.3.cloned.1.call-start = ((), (), s32[]{:S(2)}) async-start(), calls=%async_computation.3 | async-start | bytes 28311552 | tf_op jit(solution)/shard_map/all_gather | solution.py:38
  74.8 6853.9 %reduce-scatter.2.cloned.1.call-start = ((), (), s32[]{:S(2)}) async-start(), calls=%async_computation.1 | async-start | bytes 56623104 | tf_op jit(solution)/shard_map/reduce_scatter | solution.py:122
  75.4 8.8 copy-start.7
  84.2 6.9 copy-start.5
  87.2 6.9 copy-start.8
  87.2 6.9 copy-start.10
  87.2 6.9 copy-start.11
  228.2 266.1 %collective-permute-start = (bf16[384,32,128]{2,0,1:T(8,128)(2,1)}, bf16[384,32,128]{2,0,1:T(8,128)(2,1)}, u32[]{:S(2)}, u32[]{:S(2)}) collective-permute-start(bf16[384,32,128]{2,0,1:T(8,128)(2,1)} %copy.199), channel_id=1, source_target_pairs={{0,1},{1,2},{2,3},{3,4},{4,5},{5,6},{6,7},{7,0}} | collective-permute-start | bytes 9437192 | tf_op jit(solution)/shard_map/while/body/eval_jaxpr/ppermute | solution.py:69
  232.3 262.0 %collective-permute-start.1 = (bf16[384,32,128]{2,0,1:T(8,128)(2,1)}, bf16[384,32,128]{2,0,1:T(8,128)(2,1)}, u32[]{:S(2)}, u32[]{:S(2)}) collective-permute-start(bf16[384,32,128]{2,0,1:T(8,128)(2,1)} %copy.200), channel_id=1, source_target_pairs={{0,1},{1,2},{2,3},{3,4},{4,5},{5,6},{6,7},{7,0}} | collective-permute-start | bytes 9437192 | tf_op jit(solution)/shard_map/while/body/eval_jaxpr/ppermute | solution.py:70
  498.2 37.6 collective-permute-start
  502.3 67.2 collective-permute-start.1
  573.4 215.1 %collective-permute-start = (bf16[384,32,128]{2,0,1:T(8,128)(2,1)}, bf16[384,32,128]{2,0,1:T(8,128)(2,1)}, u32[]{:S(2)}, u32[]{:S(2)}) collective-permute-start(bf16[384,32,128]{2,0,1:T(8,128)(2,1)} %copy.199), channel_id=1, source_target_pairs={{0,1},{1,2},{2,3},{3,4},{4,5},{5,6},{6,7},{7,0}} | collective-permute-start | bytes 9437192 | tf_op jit(solution)/shard_map/while/body/eval_jaxpr/ppermute | solution.py:69
  754.8 67.4 collective-permute-start.1
  826.1 214.9 %collective-permute-start = (bf16[384,32,128]{2,0,1:T(8,128)(2,1)}, bf16[384,32,128]{2,0,1:T(8,128)(2,1)}, u32[]{:S(2)}, u32[]{:S(2)}) collective-permute-start(bf16[384,32,128]{2,0,1:T(8,128)(2,1)} %copy.199), channel_id=1, source_target_pairs={{0,1},{1,2},{2,3},{3,4},{4,5},{5,6},{6,7},{7,0}} | collective-permute-start | bytes 9437192 | tf_op jit(solution)/shard_map/while/body/eval_jaxpr/ppermute | solution.py:69
  830.0 244.7 %collective-permute-start.1 = (bf16[384,32,128]{2,0,1:T(8,128)(2,1)}, bf16[384,32,128]{2,0,1:T(8,128)(2,1)}, u32[]{:S(2)}, u32[]{:S(2)}) collective-permute-start(bf16[384,32,128]{2,0,1:T(8,128)(2,1)} %copy.200), channel_id=1, source_target_pairs={{0,1},{1,2},{2,3},{3,4},{4,5},{5,6},{6,7},{7,0}} | collective-permute-start | bytes 9437192 | tf_op jit(solution)/shard_map/while/body/eval_jaxpr/ppermute | solution.py:70
  1078.6 214.9 %collective-permute-start = (bf16[384,32,128]{2,0,1:T(8,128)(2,1)}, bf16[384,32,128]{2,0,1:T(8,128)(2,1)}, u32[]{:S(2)}, u32[]{:S(2)}) collective-permute-start(bf16[384,32,128]{2,0,1:T(8,128)(2,1)} %copy.199), channel_id=1, source_target_pairs={{0,1},{1,2},{2,3},{3,4},{4,5},{5,6},{6,7},{7,0}} | collective-permute-start | bytes 9437192 | tf_op jit(solution)/shard_map/while/body/eval_jaxpr/ppermute | solution.py:69
  1082.5 244.7 %collective-permute-start.1 = (bf16[384,32,128]{2,0,1:T(8,128)(2,1)}, bf16[384,32,128]{2,0,1:T(8,128)(2,1)}, u32[]{:S(2)}, u32[]{:S(2)}) collective-permute-start(bf16[384,32,128]{2,0,1:T(8,128)(2,1)} %copy.200), channel_id=1, source_target_pairs={{0,1},{1,2},{2,3},{3,4},{4,5},{5,6},{6,7},{7,0}} | collective-permute-start | bytes 9437192 | tf_op jit(solution)/shard_map/while/body/eval_jaxpr/ppermute | solution.py:70
  1331.1 214.9 %collective-permute-start = (bf16[384,32,128]{2,0,1:T(8,128)(2,1)}, bf16[384,32,128]{2,0,1:T(8,128)(2,1)}, u32[]{:S(2)}, u32[]{:S(2)}) collective-permute-start(bf16[384,32,128]{2,0,1:T(8,128)(2,1)} %copy.199), channel_id=1, source_target_pairs={{0,1},{1,2},{2,3},{3,4},{4,5},{5,6},{6,7},{7,0}} | collective-permute-start | bytes 9437192 | tf_op jit(solution)/shard_map/while/body/eval_jaxpr/ppermute | solution.py:69
  1335.0 244.7 %collective-permute-start.1 = (bf16[384,32,128]{2,0,1:T(8,128)(2,1)}, bf16[384,32,128]{2,0,1:T(8,128)(2,1)}, u32[]{:S(2)}, u32[]{:S(2)}) collective-permute-start(bf16[384,32,128]{2,0,1:T(8,128)(2,1)} %copy.200), channel_id=1, source_target_pairs={{0,1},{1,2},{2,3},{3,4},{4,5},{5,6},{6,7},{7,0}} | collective-permute-start | bytes 9437192 | tf_op jit(solution)/shard_map/while/body/eval_jaxpr/ppermute | solution.py:70
  1583.6 214.9 %collective-permute-start = (bf16[384,32,128]{2,0,1:T(8,128)(2,1)}, bf16[384,32,128]{2,0,1:T(8,128)(2,1)}, u32[]{:S(2)}, u32[]{:S(2)}) collective-permute-start(bf16[384,32,128]{2,0,1:T(8,128)(2,1)} %copy.199), channel_id=1, source_target_pairs={{0,1},{1,2},{2,3},{3,4},{4,5},{5,6},{6,7},{7,0}} | collective-permute-start | bytes 9437192 | tf_op jit(solution)/shard_map/while/body/eval_jaxpr/ppermute | solution.py:69
  1587.5 244.7 %collective-permute-start.1 = (bf16[384,32,128]{2,0,1:T(8,128)(2,1)}, bf16[384,32,128]{2,0,1:T(8,128)(2,1)}, u32[]{:S(2)}, u32[]{:S(2)}) collective-permute-start(bf16[384,32,128]{2,0,1:T(8,128)(2,1)} %copy.200), channel_id=1, source_target_pairs={{0,1},{1,2},{2,3},{3,4},{4,5},{5,6},{6,7},{7,0}} | collective-permute-start | bytes 9437192 | tf_op jit(solution)/shard_map/while/body/eval_jaxpr/ppermute | solution.py:70
  2102.6 13.5 copy-start.1
  2189.3 7.1 copy-start.3
  2225.1 8.7 copy-start.2
  2252.9 478.5 %collective-permute-start.4 = (f32[384,32,128]{2,0,1:T(8,128)}, f32[384,32,128]{2,0,1:T(8,128)}, u32[]{:S(2)}, u32[]{:S(2)}) collective-permute-start(f32[384,32,128]{2,0,1:T(8,128)} %get-tuple-element.1176), channel_id=1, source_target_pairs={{0,1},{1,2},{2,3},{3,4},{4,5},{5,6},{6,7},{7,0}} | collective-permute-start | bytes 18874376 | tf_op jit(solution)/shard_map/while/body/eval_jaxpr/ppermute | solution.py:111
  2252.9 545.9 %collective-permute-start.5 = (f32[384,32,128]{2,0,1:T(8,128)}, f32[384,32,128]{2,0,1:T(8,128)}, u32[]{:S(2)}, u32[]{:S(2)}) collective-permute-start(f32[384,32,128]{2,0,1:T(8,128)} %get-tuple-element.1177), channel_id=1, source_target_pairs={{0,1},{1,2},{2,3},{3,4},{4,5},{5,6},{6,7},{7,0}} | collective-permute-start | bytes 18874376 | tf_op jit(solution)/shard_map/while/body/eval_jaxpr/ppermute | solution.py:112
  2252.9 579.5 %collective-permute-start.2 = (bf16[384,32,128]{2,0,1:T(8,128)(2,1)}, bf16[384,32,128]{2,0,1:T(8,128)(2,1)}, u32[]{:S(2)}, u32[]{:S(2)}) collective-permute-start(bf16[384,32,128]{2,0,1:T(8,128)(2,1)} %copy.225), channel_id=1, source_target_pairs={{0,1},{1,2},{2,3},{3,4},{4,5},{5,6},{6,7},{7,0}} | collective-permute-start | bytes 9437192 | tf_op jit(solution)/shard_map/while/body/eval_jaxpr/ppermute | solution.py:109
  2253.0 613.2 %collective-permute-start.3 = (bf16[384,32,128]{2,0,1:T(8,128)(2,1)}, bf16[384,32,128]{2,0,1:T(8,128)(2,1)}, u32[]{:S(2)}, u32[]{:S(2)}) collective-permute-start(bf16[384,32,128]{2,0,1:T(8,128)(2,1)} %copy.226), channel_id=1, source_target_pairs={{0,1},{1,2},{2,3},{3,4},{4,5},{5,6},{6,7},{7,0}} | collective-permute-start | bytes 9437192 | tf_op jit(solution)/shard_map/while/body/eval_jaxpr/ppermute | solution.py:110
  2877.9 424.1 %collective-permute-start.4 = (f32[384,32,128]{2,0,1:T(8,128)}, f32[384,32,128]{2,0,1:T(8,128)}, u32[]{:S(2)}, u32[]{:S(2)}) collective-permute-start(f32[384,32,128]{2,0,1:T(8,128)} %get-tuple-element.1176), channel_id=1, source_target_pairs={{0,1},{1,2},{2,3},{3,4},{4,5},{5,6},{6,7},{7,0}} | collective-permute-start | bytes 18874376 | tf_op jit(solution)/shard_map/while/body/eval_jaxpr/ppermute | solution.py:111
  2877.9 491.5 %collective-permute-start.5 = (f32[384,32,128]{2,0,1:T(8,128)}, f32[384,32,128]{2,0,1:T(8,128)}, u32[]{:S(2)}, u32[]{:S(2)}) collective-permute-start(f32[384,32,128]{2,0,1:T(8,128)} %get-tuple-element.1177), channel_id=1, source_target_pairs={{0,1},{1,2},{2,3},{3,4},{4,5},{5,6},{6,7},{7,0}} | collective-permute-start | bytes 18874376 | tf_op jit(solution)/shard_map/while/body/eval_jaxpr/ppermute | solution.py:112
  2878.0 525.2 %collective-permute-start.2 = (bf16[384,32,128]{2,0,1:T(8,128)(2,1)}, bf16[384,32,128]{2,0,1:T(8,128)(2,1)}, u32[]{:S(2)}, u32[]{:S(2)}) collective-permute-start(bf16[384,32,128]{2,0,1:T(8,128)(2,1)} %copy.225), channel_id=1, source_target_pairs={{0,1},{1,2},{2,3},{3,4},{4,5},{5,6},{6,7},{7,0}} | collective-permute-start | bytes 9437192 | tf_op jit(solution)/shard_map/while/body/eval_jaxpr/ppermute | solution.py:109
  3068.1 368.8 %collective-permute-start.3 = (bf16[384,32,128]{2,0,1:T(8,128)(2,1)}, bf16[384,32,128]{2,0,1:T(8,128)(2,1)}, u32[]{:S(2)}, u32[]{:S(2)}) collective-permute-start(bf16[384,32,128]{2,0,1:T(8,128)(2,1)} %copy.226), channel_id=1, source_target_pairs={{0,1},{1,2},{2,3},{3,4},{4,5},{5,6},{6,7},{7,0}} | collective-permute-start | bytes 9437192 | tf_op jit(solution)/shard_map/while/body/eval_jaxpr/ppermute | solution.py:110
  3446.6 426.4 %collective-permute-start.4 = (f32[384,32,128]{2,0,1:T(8,128)}, f32[384,32,128]{2,0,1:T(8,128)}, u32[]{:S(2)}, u32[]{:S(2)}) collective-permute-start(f32[384,32,128]{2,0,1:T(8,128)} %get-tuple-element.1176), channel_id=1, source_target_pairs={{0,1},{1,2},{2,3},{3,4},{4,5},{5,6},{6,7},{7,0}} | collective-permute-start | bytes 18874376 | tf_op jit(solution)/shard_map/while/body/eval_jaxpr/ppermute | solution.py:111
  3446.6 493.8 %collective-permute-start.5 = (f32[384,32,128]{2,0,1:T(8,128)}, f32[384,32,128]{2,0,1:T(8,128)}, u32[]{:S(2)}, u32[]{:S(2)}) collective-permute-start(f32[384,32,128]{2,0,1:T(8,128)} %get-tuple-element.1177), channel_id=1, source_target_pairs={{0,1},{1,2},{2,3},{3,4},{4,5},{5,6},{6,7},{7,0}} | collective-permute-start | bytes 18874376 | tf_op jit(solution)/shard_map/while/body/eval_jaxpr/ppermute | solution.py:112
  3573.9 400.2 %collective-permute-start.2 = (bf16[384,32,128]{2,0,1:T(8,128)(2,1)}, bf16[384,32,128]{2,0,1:T(8,128)(2,1)}, u32[]{:S(2)}, u32[]{:S(2)}) collective-permute-start(bf16[384,32,128]{2,0,1:T(8,128)(2,1)} %copy.225), channel_id=1, source_target_pairs={{0,1},{1,2},{2,3},{3,4},{4,5},{5,6},{6,7},{7,0}} | collective-permute-start | bytes 9437192 | tf_op jit(solution)/shard_map/while/body/eval_jaxpr/ppermute | solution.py:109
  3672.5 335.3 %collective-permute-start.3 = (bf16[384,32,128]{2,0,1:T(8,128)(2,1)}, bf16[384,32,128]{2,0,1:T(8,128)(2,1)}, u32[]{:S(2)}, u32[]{:S(2)}) collective-permute-start(bf16[384,32,128]{2,0,1:T(8,128)(2,1)} %copy.226), channel_id=1, source_target_pairs={{0,1},{1,2},{2,3},{3,4},{4,5},{5,6},{6,7},{7,0}} | collective-permute-start | bytes 9437192 | tf_op jit(solution)/shard_map/while/body/eval_jaxpr/ppermute | solution.py:110
  4017.4 426.6 %collective-permute-start.4 = (f32[384,32,128]{2,0,1:T(8,128)}, f32[384,32,128]{2,0,1:T(8,128)}, u32[]{:S(2)}, u32[]{:S(2)}) collective-permute-start(f32[384,32,128]{2,0,1:T(8,128)} %get-tuple-element.1176), channel_id=1, source_target_pairs={{0,1},{1,2},{2,3},{3,4},{4,5},{5,6},{6,7},{7,0}} | collective-permute-start | bytes 18874376 | tf_op jit(solution)/shard_map/while/body/eval_jaxpr/ppermute | solution.py:111
  4017.4 494.0 %collective-permute-start.5 = (f32[384,32,128]{2,0,1:T(8,128)}, f32[384,32,128]{2,0,1:T(8,128)}, u32[]{:S(2)}, u32[]{:S(2)}) collective-permute-start(f32[384,32,128]{2,0,1:T(8,128)} %get-tuple-element.1177), channel_id=1, source_target_pairs={{0,1},{1,2},{2,3},{3,4},{4,5},{5,6},{6,7},{7,0}} | collective-permute-start | bytes 18874376 | tf_op jit(solution)/shard_map/while/body/eval_jaxpr/ppermute | solution.py:112
  4017.4 527.7 %collective-permute-start.2 = (bf16[384,32,128]{2,0,1:T(8,128)(2,1)}, bf16[384,32,128]{2,0,1:T(8,128)(2,1)}, u32[]{:S(2)}, u32[]{:S(2)}) collective-permute-start(bf16[384,32,128]{2,0,1:T(8,128)(2,1)} %copy.225), channel_id=1, source_target_pairs={{0,1},{1,2},{2,3},{3,4},{4,5},{5,6},{6,7},{7,0}} | collective-permute-start | bytes 9437192 | tf_op jit(solution)/shard_map/while/body/eval_jaxpr/ppermute | solution.py:109
  4246.9 331.9 %collective-permute-start.3 = (bf16[384,32,128]{2,0,1:T(8,128)(2,1)}, bf16[384,32,128]{2,0,1:T(8,128)(2,1)}, u32[]{:S(2)}, u32[]{:S(2)}) collective-permute-start(bf16[384,32,128]{2,0,1:T(8,128)(2,1)} %copy.226), channel_id=1, source_target_pairs={{0,1},{1,2},{2,3},{3,4},{4,5},{5,6},{6,7},{7,0}} | collective-permute-start | bytes 9437192 | tf_op jit(solution)/shard_map/while/body/eval_jaxpr/ppermute | solution.py:110
  4588.3 426.8 %collective-permute-start.4 = (f32[384,32,128]{2,0,1:T(8,128)}, f32[384,32,128]{2,0,1:T(8,128)}, u32[]{:S(2)}, u32[]{:S(2)}) collective-permute-start(f32[384,32,128]{2,0,1:T(8,128)} %get-tuple-element.1176), channel_id=1, source_target_pairs={{0,1},{1,2},{2,3},{3,4},{4,5},{5,6},{6,7},{7,0}} | collective-permute-start | bytes 18874376 | tf_op jit(solution)/shard_map/while/body/eval_jaxpr/ppermute | solution.py:111
  4588.3 494.2 %collective-permute-start.5 = (f32[384,32,128]{2,0,1:T(8,128)}, f32[384,32,128]{2,0,1:T(8,128)}, u32[]{:S(2)}, u32[]{:S(2)}) collective-permute-start(f32[384,32,128]{2,0,1:T(8,128)} %get-tuple-element.1177), channel_id=1, source_target_pairs={{0,1},{1,2},{2,3},{3,4},{4,5},{5,6},{6,7},{7,0}} | collective-permute-start | bytes 18874376 | tf_op jit(solution)/shard_map/while/body/eval_jaxpr/ppermute | solution.py:112
  4588.3 527.9 %collective-permute-start.2 = (bf16[384,32,128]{2,0,1:T(8,128)(2,1)}, bf16[384,32,128]{2,0,1:T(8,128)(2,1)}, u32[]{:S(2)}, u32[]{:S(2)}) collective-permute-start(bf16[384,32,128]{2,0,1:T(8,128)(2,1)} %copy.225), channel_id=1, source_target_pairs={{0,1},{1,2},{2,3},{3,4},{4,5},{5,6},{6,7},{7,0}} | collective-permute-start | bytes 9437192 | tf_op jit(solution)/shard_map/while/body/eval_jaxpr/ppermute | solution.py:109
  4588.4 561.6 %collective-permute-start.3 = (bf16[384,32,128]{2,0,1:T(8,128)(2,1)}, bf16[384,32,128]{2,0,1:T(8,128)(2,1)}, u32[]{:S(2)}, u32[]{:S(2)}) collective-permute-start(bf16[384,32,128]{2,0,1:T(8,128)(2,1)} %copy.226), channel_id=1, source_target_pairs={{0,1},{1,2},{2,3},{3,4},{4,5},{5,6},{6,7},{7,0}} | collective-permute-start | bytes 9437192 | tf_op jit(solution)/shard_map/while/body/eval_jaxpr/ppermute | solution.py:110
  5159.5 426.3 %collective-permute-start.4 = (f32[384,32,128]{2,0,1:T(8,128)}, f32[384,32,128]{2,0,1:T(8,128)}, u32[]{:S(2)}, u32[]{:S(2)}) collective-permute-start(f32[384,32,128]{2,0,1:T(8,128)} %get-tuple-element.1176), channel_id=1, source_target_pairs={{0,1},{1,2},{2,3},{3,4},{4,5},{5,6},{6,7},{7,0}} | collective-permute-start | bytes 18874376 | tf_op jit(solution)/shard_map/while/body/eval_jaxpr/ppermute | solution.py:111
  5159.5 493.7 %collective-permute-start.5 = (f32[384,32,128]{2,0,1:T(8,128)}, f32[384,32,128]{2,0,1:T(8,128)}, u32[]{:S(2)}, u32[]{:S(2)}) collective-permute-start(f32[384,32,128]{2,0,1:T(8,128)} %get-tuple-element.1177), channel_id=1, source_target_pairs={{0,1},{1,2},{2,3},{3,4},{4,5},{5,6},{6,7},{7,0}} | collective-permute-start | bytes 18874376 | tf_op jit(solution)/shard_map/while/body/eval_jaxpr/ppermute | solution.py:112
  5159.6 527.4 %collective-permute-start.2 = (bf16[384,32,128]{2,0,1:T(8,128)(2,1)}, bf16[384,32,128]{2,0,1:T(8,128)(2,1)}, u32[]{:S(2)}, u32[]{:S(2)}) collective-permute-start(bf16[384,32,128]{2,0,1:T(8,128)(2,1)} %copy.225), channel_id=1, source_target_pairs={{0,1},{1,2},{2,3},{3,4},{4,5},{5,6},{6,7},{7,0}} | collective-permute-start | bytes 9437192 | tf_op jit(solution)/shard_map/while/body/eval_jaxpr/ppermute | solution.py:109
  5159.6 561.1 %collective-permute-start.3 = (bf16[384,32,128]{2,0,1:T(8,128)(2,1)}, bf16[384,32,128]{2,0,1:T(8,128)(2,1)}, u32[]{:S(2)}, u32[]{:S(2)}) collective-permute-start(bf16[384,32,128]{2,0,1:T(8,128)(2,1)} %copy.226), channel_id=1, source_target_pairs={{0,1},{1,2},{2,3},{3,4},{4,5},{5,6},{6,7},{7,0}} | collective-permute-start | bytes 9437192 | tf_op jit(solution)/shard_map/while/body/eval_jaxpr/ppermute | solution.py:110
  5730.2 426.5 %collective-permute-start.4 = (f32[384,32,128]{2,0,1:T(8,128)}, f32[384,32,128]{2,0,1:T(8,128)}, u32[]{:S(2)}, u32[]{:S(2)}) collective-permute-start(f32[384,32,128]{2,0,1:T(8,128)} %get-tuple-element.1176), channel_id=1, source_target_pairs={{0,1},{1,2},{2,3},{3,4},{4,5},{5,6},{6,7},{7,0}} | collective-permute-start | bytes 18874376 | tf_op jit(solution)/shard_map/while/body/eval_jaxpr/ppermute | solution.py:111
  5730.2 493.9 %collective-permute-start.5 = (f32[384,32,128]{2,0,1:T(8,128)}, f32[384,32,128]{2,0,1:T(8,128)}, u32[]{:S(2)}, u32[]{:S(2)}) collective-permute-start(f32[384,32,128]{2,0,1:T(8,128)} %get-tuple-element.1177), channel_id=1, source_target_pairs={{0,1},{1,2},{2,3},{3,4},{4,5},{5,6},{6,7},{7,0}} | collective-permute-start | bytes 18874376 | tf_op jit(solution)/shard_map/while/body/eval_jaxpr/ppermute | solution.py:112
  5730.3 527.7 %collective-permute-start.2 = (bf16[384,32,128]{2,0,1:T(8,128)(2,1)}, bf16[384,32,128]{2,0,1:T(8,128)(2,1)}, u32[]{:S(2)}, u32[]{:S(2)}) collective-permute-start(bf16[384,32,128]{2,0,1:T(8,128)(2,1)} %copy.225), channel_id=1, source_target_pairs={{0,1},{1,2},{2,3},{3,4},{4,5},{5,6},{6,7},{7,0}} | collective-permute-start | bytes 9437192 | tf_op jit(solution)/shard_map/while/body/eval_jaxpr/ppermute | solution.py:109
  5730.3 561.3 %collective-permute-start.3 = (bf16[384,32,128]{2,0,1:T(8,128)(2,1)}, bf16[384,32,128]{2,0,1:T(8,128)(2,1)}, u32[]{:S(2)}, u32[]{:S(2)}) collective-permute-start(bf16[384,32,128]{2,0,1:T(8,128)(2,1)} %copy.226), channel_id=1, source_target_pairs={{0,1},{1,2},{2,3},{3,4},{4,5},{5,6},{6,7},{7,0}} | collective-permute-start | bytes 9437192 | tf_op jit(solution)/shard_map/while/body/eval_jaxpr/ppermute | solution.py:110
  6312.0 1508.9 %all-reduce.7.cloned.1.call-start = ((), (), s32[]{:S(2)}) async-start(), calls=%async_computation.2 | async-start | bytes 134217728 | tf_op jit(solution)/shard_map/psum | solution.py:124
  7013.3 232.9 %collective-permute-start.6 = (bf16[384,32,128]{2,1,0:T(8,128)(2,1)}, bf16[384,32,128]{2,1,0:T(8,128)(2,1)}, u32[]{:S(2)}, u32[]{:S(2)}) collective-permute-start(bf16[384,32,128]{2,1,0:T(8,128)(2,1)} %copy.118), channel_id=1, source_target_pairs={{0,1},{1,2},{2,3},{3,4},{4,5},{5,6},{6,7},{7,0}} | collective-permute-start | bytes 9437192 | tf_op jit(solution)/shard_map/ppermute | solution.py:120
  7021.4 224.8 %collective-permute-start.7 = (bf16[384,32,128]{2,1,0:T(8,128)(2,1)}, bf16[384,32,128]{2,1,0:T(8,128)(2,1)}, u32[]{:S(2)}, u32[]{:S(2)}) collective-permute-start(bf16[384,32,128]{2,1,0:T(8,128)(2,1)} %copy.119), channel_id=1, source_target_pairs={{0,1},{1,2},{2,3},{3,4},{4,5},{5,6},{6,7},{7,0}} | collective-permute-start | bytes 9437192 | tf_op jit(solution)/shard_map/ppermute | solution.py:121
Sparse Core Ops, SparseCore 0:
  75.0 122.4 all-gather.2
  6312.1 616.5 reduce-scatter.1
  7005.4 815.5 all-reduce.6
where the time goes:
time: 7940 us; the launch traced here: 7900 us
  waiting for transfers between devices  5220 us (66%)
  starting transfers between devices  1270 us (16%)
  local copies, waits for them, and re-layouts  905 us (11%)
  matrix products  207 us (3%)
  blocking collectives  200 us (3%)
    ppermute x7, waiting for transfers between devices, bwd_step(): dk_acc = lax.ppermute(dk_acc, 'cp', shift_pairs)  2140 us
    ppermute x7, waiting for transfers between devices, fwd_step(): k_blk = lax.ppermute(k_blk, 'cp', shift_pairs)  724 us
    reduce_scatter x1, waiting for transfers between devices, local_fn(): lax.psum_scatter(grad_rel, 'cp', scatter_dimension=0, tiled=False)  617 us
    psum x1, waiting for transfers between devices, local_fn(): lax.psum(jnp.einsum('uo,ujf->ojf', rel_table, d_rel, preferred_element_ty...  575 us
    ppermute x7, starting transfers between devices, bwd_step(): k_blk = lax.ppermute(k_blk, 'cp', shift_pairs)  518 us
    ppermute x7, waiting for transfers between devices, bwd_step(): dv_acc = lax.ppermute(dv_acc, 'cp', shift_pairs)  429 us
    ppermute x7, starting transfers between devices, bwd_step(): v_blk = lax.ppermute(v_blk, 'cp', shift_pairs)  247 us
    ppermute x7, waiting for transfers between devices, bwd_step(): v_blk = lax.ppermute(v_blk, 'cp', shift_pairs)  236 us
  transfers between devices with their start and end apart: 47, of which 43 were waited for; matrix products, arithmetic and copies ran while one was open for 5% of the time, Pallas kernels for 0%

commit v1 on v0

v1 whole, which is shorter than its diff:
```python
import jax
import jax.numpy as jnp
from jax import lax
from jax.experimental import pallas as pl
from jax.experimental.pallas import tpu as pltpu
from jax.sharding import PartitionSpec as P

f32, bf16 = jnp.float32, jnp.bfloat16
VM = pl.BlockSpec(memory_space=pltpu.VMEM)
MIB = 1024 * 1024


def attn_kernel(x_ref, rel_ref, ub_ref, vb_ref, y_ref, drel_ref, du_ref, dv_ref,
                q_s, k_s, v_s, g_s, r_s, kT_s, vT_s, rT_s, dkT_s, dvT_s, drT_s, sc_s, carry_s, acc_s, dcar_s):
    T = q_s.shape[0]
    NB, _, BL, D = x_ref.shape
    Q, C = 256, 512
    nq = T // Q
    scale = D ** -0.5
    c2 = scale * 1.4426950408889634
    for b in range(NB):
        for a, dst in enumerate((q_s, k_s, v_s, g_s)):
            dst[pl.ds(b * BL, BL), :] = x_ref[b, a]
    flip8 = 7 - lax.broadcasted_iota(jnp.int32, (8, 128), 0)

    def flip(x):
        n, w = x.shape
        rows = []
        for g in range(n // 8 - 1, -1, -1):
            rows.append(jnp.concatenate([jnp.take_along_axis(x[8 * g:8 * g + 8, 128 * t:128 * t + 128], flip8, axis=0) for t in range(w // 128)], axis=1))
        return jnp.concatenate(rows, axis=0)

    def flip_rel(c, _):
        o = pl.multiple_of(c * Q, Q)
        r_s[pl.ds(pl.multiple_of(T - Q - c * Q, Q), Q), :] = flip(rel_ref[pl.ds(o, Q), :].astype(f32)).astype(bf16)
        return 0
    lax.fori_loop(0, nq, flip_rel, 0)
    r_s[pl.ds(T, Q), :] = jnp.zeros((Q, D), bf16)
    def tr(c, _):
        o = pl.multiple_of(c * Q, Q)
        for src, dst in ((k_s, kT_s), (v_s, vT_s), (r_s, rT_s)):
            dst[:, pl.ds(o, Q)] = src[pl.ds(o, Q), :].astype(f32).T.astype(bf16)
        for dst in (dkT_s, dvT_s, drT_s):
            dst[:, pl.ds(o, Q)] = jnp.zeros((D, Q), f32)
        return 0
    lax.fori_loop(0, nq, tr, 0)
    rT_s[:, pl.ds(T, Q)] = jnp.zeros((D, Q), bf16)
    drT_s[:, pl.ds(T, Q)] = jnp.zeros((D, Q), f32)
    du_ref[...] = jnp.zeros_like(du_ref)
    dv_ref[...] = jnp.zeros_like(dv_ref)
    def qblock(i, _):
        i0 = pl.multiple_of(i * Q, Q)
        nk = (i + 2) // 2
        w0 = T - Q - i0
        qf = q_s[pl.ds(i0, Q), :].astype(f32)
        quf = (qf + ub_ref[...]).astype(bf16).astype(f32)
        qvf = (qf + vb_ref[...]).astype(bf16).astype(f32)
        qu, qv = quf.astype(bf16), qvf.astype(bf16)
        do = g_s[pl.ds(i0, Q), :]
        dof = do.astype(f32)
        lane = lax.broadcasted_iota(jnp.int32, (Q, Q), 1)
        row = lax.broadcasted_iota(jnp.int32, (Q, Q), 0)
        low = lane < row + 1

        def scores(t, mrun, diag):
            o = pl.multiple_of(t * C, C)
            w = pl.multiple_of(w0 + o, Q)
            b = jnp.dot(qv, rT_s[:, pl.ds(w, C)], preferred_element_type=f32)
            rolled = pltpu.roll(b, C - (Q - 1), 1, stride=1, stride_axis=0)
            right = rolled[:, Q:]
            if diag:
                pos = rolled
            else:
                pos = jnp.concatenate([rolled[:, :Q], jnp.where(low, right, carry_s[...])], axis=1)
            carry_s[...] = right
            s = jnp.dot(qu, kT_s[:, pl.ds(o, C)], preferred_element_type=f32) + pos
            if diag:
                jj = o + lax.broadcasted_iota(jnp.int32, (Q, C), 1)
                ii = i0 + lax.broadcasted_iota(jnp.int32, (Q, C), 0)
                s = jnp.where(jj <= ii, s, -jnp.inf)
            sc_s[:, pl.ds(o, C)] = s
            for u in range(C // 128):
                mrun = jnp.maximum(mrun, s[:, 128 * u:128 * u + 128])
            return mrun
        mrun = scores(nk - 1, jnp.full((Q, 128), -jnp.inf, f32), True)
        mrun = lax.fori_loop(1, nk, lambda tt, m: scores(nk - 1 - tt, m, False), mrun)
        m = jnp.broadcast_to(jnp.max(mrun, axis=1, keepdims=True), (Q, 128))

        def probs(t, st):
            lrun, oacc = st
            o = pl.multiple_of(t * C, C)
            p = []
            for u in range(C // 128):
                pu = jnp.exp2((sc_s[:, pl.ds(o + 128 * u, 128)] - m) * c2)
                lrun = lrun + pu
                sc_s[:, pl.ds(o + 128 * u, 128)] = pu
                p.append(pu.astype(bf16))
            oacc = oacc + jnp.dot(jnp.concatenate(p, axis=1), v_s[pl.ds(o, C), :], preferred_element_type=f32)
            return lrun, oacc
        lrun, oacc = lax.fori_loop(0, nk, probs, (jnp.zeros((Q, 128), f32), jnp.zeros((Q, D), f32)))
        rl = jnp.broadcast_to(1.0 / jnp.sum(lrun, axis=1, keepdims=True), (Q, 128))
        out = oacc * rl
        delta = jnp.broadcast_to(jnp.sum(dof * out, axis=1, keepdims=True), (Q, 128))
        def put(a, val):
            for h in range(Q // 128):
                r0 = i0 + 128 * h
                y_ref[r0 // BL, a, pl.ds(pl.multiple_of(r0 % BL, 128), 128), :] = val[128 * h:128 * h + 128]
        put(0, out.astype(bf16))
        doT, quT = dof.T.astype(bf16), quf.T.astype(bf16)
        qvrT = flip(qvf).T.astype(bf16)
        geq = lane >= row
        dcar_s[...] = jnp.zeros((Q, Q), f32)

        def grads(t, st):
            dqu, dqv = st
            o = pl.multiple_of(t * C, C)
            w = pl.multiple_of(w0 + o, Q)
            dp = jnp.dot(do, vT_s[:, pl.ds(o, C)], preferred_element_type=f32)
            pb, ds = [], []
            for u in range(C // 128):
                pu = sc_s[:, pl.ds(o + 128 * u, 128)] * rl
                pb.append(pu.astype(bf16))
                ds.append(pu * (dp[:, 128 * u:128 * u + 128] - delta))
            pb = jnp.concatenate(pb, axis=1)
            ds = jnp.concatenate(ds, axis=1)
            dsb = ds.astype(bf16)
            dvT_s[:, pl.ds(o, C)] += jnp.dot(doT, pb, preferred_element_type=f32)
            dkT_s[:, pl.ds(o, C)] += jnp.dot(quT, dsb, preferred_element_type=f32)
            dqu = dqu + jnp.dot(dsb, k_s[pl.ds(o, C), :], preferred_element_type=f32)
            rolled = pltpu.roll(flip(ds), 0, 1, stride=1, stride_axis=0)
            left = rolled[:, :Q]
            dw = jnp.concatenate([jnp.where(geq, left, dcar_s[...]), rolled[:, Q:]], axis=1).astype(bf16)
            dcar_s[...] = left
            dqv = dqv + jnp.dot(dw, r_s[pl.ds(w, C), :], preferred_element_type=f32)
            drT_s[:, pl.ds(w, C)] += jnp.dot(qvrT, dw, preferred_element_type=f32)
            return dqu, dqv
        dqu, dqv = lax.fori_loop(0, nk, grads, (jnp.zeros((Q, D), f32), jnp.zeros((Q, D), f32)))
        dqu = dqu * scale
        dqv = flip(dqv) * scale
        put(1, (dqu + dqv).astype(bf16))
        du_ref[...] += jnp.sum(dqu, axis=0, keepdims=True)
        dv_ref[...] += jnp.sum(dqv, axis=0, keepdims=True)
        return 0
    lax.fori_loop(0, nq, qblock, 0)
    for b in range(NB):
        y_ref[b, 2] = (dkT_s[:, pl.ds(b * BL, BL)] * scale).T.astype(bf16)
        y_ref[b, 3] = dvT_s[:, pl.ds(b * BL, BL)].T.astype(bf16)

    def unflip_rel(c, _):
        o = pl.multiple_of(c * Q, Q)
        drel_ref[pl.ds(pl.multiple_of(T - Q - c * Q, Q), Q), :] = flip((drT_s[:, pl.ds(o, Q)] * scale).T).astype(bf16)
        return 0
    lax.fori_loop(0, nq, unflip_rel, 0)

def attn(x, relf, ub, vb):
    NB, _, BL, D = x.shape
    T = NB * BL
    vm = pl.BlockSpec(memory_space=pltpu.VMEM)
    flops = 9 * 2 * T * T // 2 * D
    return pl.pallas_call(
        attn_kernel,
        out_shape=(jax.ShapeDtypeStruct(x.shape, bf16), jax.ShapeDtypeStruct((T, D), bf16),
                   jax.ShapeDtypeStruct((1, D), f32), jax.ShapeDtypeStruct((1, D), f32)),
        in_specs=[vm] * 4, out_specs=(vm,) * 4,
        scratch_shapes=[pltpu.VMEM((T, D), bf16)] * 4 + [pltpu.VMEM((T + 256, D), bf16)]
        + [pltpu.VMEM((D, T), bf16)] * 2 + [pltpu.VMEM((D, T + 256), bf16)]
        + [pltpu.VMEM((D, T), f32)] * 2 + [pltpu.VMEM((D, T + 256), f32)]
        + [pltpu.VMEM((256, T), f32), pltpu.VMEM((256, 256), f32), pltpu.VMEM((256, 256), f32), pltpu.VMEM((256, 256), f32)],
        compiler_params=pltpu.CompilerParams(vmem_limit_bytes=56 * 1024 * 1024),
        cost_estimate=pl.CostEstimate(flops=flops, bytes_accessed=8 * T * D * 2, transcendentals=T * T // 2),
    )(x, relf, ub, vb)


def split_kernel(q_ref, k_ref, v_ref, g_ref, x_ref, buf):
    BL, HB, D = q_ref.shape
    for a, src in enumerate((q_ref, k_ref, v_ref, g_ref)):
        buf[...] = src[...].astype(f32).reshape(BL * HB, D)
        for h in range(HB):
            x_ref[h, a] = buf[pl.ds(h, BL, stride=HB), :].astype(bf16)


def split_heads(q, k, v, g, step, n_dev):
    BL, _, D = q.shape
    return pl.pallas_call(
        split_kernel,
        grid=(1,),
        out_shape=jax.ShapeDtypeStruct((n_dev, 4, BL, D), bf16),
        in_specs=[pl.BlockSpec((BL, n_dev, D), lambda i: (0, step, 0))] * 4,
        out_specs=pl.BlockSpec((n_dev, 4, BL, D), lambda i: (0, 0, 0, 0)),
        scratch_shapes=[pltpu.VMEM((BL * n_dev, D), f32)],
        compiler_params=pltpu.CompilerParams(vmem_limit_bytes=40 * MIB),
        cost_estimate=pl.CostEstimate(flops=10 ** 8, bytes_accessed=16 * n_dev * BL * D, transcendentals=0),
    )(q, k, v, g)


def merge_kernel(*refs):
    z_ref, outs, buf = refs[0], refs[-5:-1], refs[-1]
    HB, _, BL, D = z_ref.shape
    for a, dst in enumerate(outs):
        for h in range(HB):
            buf[pl.ds(h, BL, stride=HB), :] = z_ref[h, a].astype(f32)
        dst[...] = buf[...].reshape(BL, HB, D).astype(bf16)


def merge_heads(z, prev, step, num_heads):
    HB, _, BL, D = z.shape
    out = jax.ShapeDtypeStruct((BL, num_heads, D), bf16)
    ops = (z,) if prev is None else (z, *prev)
    return pl.pallas_call(
        merge_kernel,
        grid=(1,),
        out_shape=(out,) * 4,
        in_specs=[pl.BlockSpec((HB, 4, BL, D), lambda i: (0, 0, 0, 0))] + [pl.BlockSpec(memory_space=pl.ANY)] * (len(ops) - 1),
        out_specs=(pl.BlockSpec((BL, HB, D), lambda i: (0, step, 0)),) * 4,
        scratch_shapes=[pltpu.VMEM((BL * HB, D), f32)],
        input_output_aliases={} if prev is None else {1: 0, 2: 1, 3: 2, 4: 3},
        compiler_params=pltpu.CompilerParams(vmem_limit_bytes=40 * MIB),
        cost_estimate=pl.CostEstimate(flops=10 ** 8, bytes_accessed=16 * HB * BL * D, transcendentals=0),
    )(*ops)


def dw_kernel(t_ref, d_ref, *rest):
    o_ref = rest[-1]
    MB, HB, D = o_ref.shape
    rhs = jnp.concatenate([d_ref[h] for h in range(HB)], axis=1)
    acc = lax.dot_general(t_ref[...], rhs, (((0,), (0,)), ((), ())), preferred_element_type=f32)
    out = o_ref.reshape(MB * HB, D)
    for h in range(HB):
        out[pl.ds(h, MB, stride=HB), :] = acc[:, h * D:(h + 1) * D]


def dw_matmul(table, drel, prev, step, num_heads):
    T, M = table.shape
    HB, _, D = drel.shape
    MB = 256
    ops = (table, drel) if prev is None else (table, drel, prev)
    return pl.pallas_call(
        dw_kernel,
        grid=(M // MB,),
        out_shape=jax.ShapeDtypeStruct((M, num_heads, D), f32),
        in_specs=[pl.BlockSpec((T, MB), lambda i: (0, i)), pl.BlockSpec((HB, T, D), lambda i: (0, 0, 0))] + [pl.BlockSpec(memory_space=pl.ANY)] * (len(ops) - 2),
        out_specs=pl.BlockSpec((MB, HB, D), lambda i: (i, step, 0)),
        input_output_aliases={} if prev is None else {2: 0},
        compiler_params=pltpu.CompilerParams(vmem_limit_bytes=56 * MIB),
        cost_estimate=pl.CostEstimate(flops=2 * T * M * HB * D, bytes_accessed=2 * T * M + 2 * T * HB * D + 4 * M * HB * D, transcendentals=0),
    )(*ops)


def rel_kernel(t_ref, w_ref, o_ref):
    o_ref[...] = jnp.dot(t_ref[...], w_ref[...], preferred_element_type=f32).astype(bf16)


def rel_matmul(table, w):
    T, M = table.shape
    N = w.shape[1]
    TB = 384
    return pl.pallas_call(
        rel_kernel,
        grid=(T // TB,),
        out_shape=jax.ShapeDtypeStruct((T, N), bf16),
        in_specs=[pl.BlockSpec((TB, M), lambda i: (i, 0)), pl.BlockSpec((M, N), lambda i: (0, 0))],
        out_specs=pl.BlockSpec((TB, N), lambda i: (i, 0)),
        compiler_params=pltpu.CompilerParams(vmem_limit_bytes=56 * MIB),
        cost_estimate=pl.CostEstimate(flops=2 * T * M * N, bytes_accessed=2 * (T * M + M * N + T * N), transcendentals=0),
    )(table, w)


def solution(mesh):
    n_dev = mesh.shape['cp']
    seq_spec = P('cp', 'hp', None)
    head_spec = P('hp', None)
    weight_spec = P(None, 'hp', None)

    def local_fn(q, k, v, u_bias, v_bias, rel_table, w_rel, d_out):
        BL, H, D = q.shape
        M = w_rel.shape[0]
        steps = H // n_dev
        me = lax.axis_index('cp')
        table = lax.all_gather(rel_table, 'cp', tiled=True)
        w_own = lax.dynamic_index_in_dim(w_rel.reshape(M, steps, n_dev, D), me, 2, keepdims=False).reshape(M, steps * D)
        ub = lax.dynamic_index_in_dim(u_bias.reshape(steps, n_dev, D), me, 1, keepdims=False)
        vb = lax.dynamic_index_in_dim(v_bias.reshape(steps, n_dev, D), me, 1, keepdims=False)
        xs = [lax.all_to_all(split_heads(q, k, v, d_out, s, n_dev), 'cp', 0, 0) for s in range(steps)]
        rel = rel_matmul(table, w_own)
        outs, dw, sums = None, None, []
        for s in range(steps):
            y, drel, du, dv = attn(xs[s], rel[:, s * D:(s + 1) * D], ub[s:s + 1], vb[s:s + 1])
            sums.append(jnp.stack([du, dv]))
            drel_all = lax.all_gather(drel, 'cp')
            z = lax.all_to_all(y, 'cp', 0, 0)
            dw = dw_matmul(table, drel_all, dw, s, H)
            outs = merge_heads(z, outs, s, H)
        sums = lax.all_gather(jnp.concatenate(sums, axis=1), 'cp')
        sums = sums.transpose(1, 2, 0, 3).reshape(2, H, D)
        return (*outs, sums[0], sums[1], dw)

    return jax.shard_map(
        local_fn,
        mesh=mesh,
        in_specs=(seq_spec, seq_spec, seq_spec, head_spec, head_spec, P('cp', None), weight_spec, seq_spec),
        out_specs=(seq_spec, seq_spec, seq_spec, seq_spec, head_spec, head_spec, weight_spec),
        check_vma=False,
    )
```

time: 7940 us -> 982 us (0.12)
  waiting for transfers between devices: 5220 us -> 111 us
  starting transfers between devices: 1270 us -> 11.1 us
  local copies, waits for them, and re-layouts: 905 us -> 56.2 us
  Pallas kernels: 0 us -> 463 us
  matrix products: 207 us -> 0 us
  blocking collectives: 200 us -> 313 us
    ppermute x44 -> x0, waiting for transfers between devices: 3930 us -> none  [the longest x7 2140 us: bwd_step(): dk_acc = lax.ppermute(dk_acc, 'cp', shift_pairs)]
    ppermute x44 -> x0, starting transfers between devices: 1270 us -> none  [the longest x7 518 us: bwd_step(): k_blk = lax.ppermute(k_blk, 'cp', shift_pairs)]
    reduce_scatter x1 -> x0, waiting for transfers between devices: 617 us -> none  [local_fn(): lax.psum_scatter(grad_rel, 'cp', scatter_dimension=0, tiled=False)]
    psum x1 -> x0, waiting for transfers between devices: 575 us -> none  [local_fn(): lax.psum(jnp.einsum('uo,ujf->ojf', rel_table, d_rel, preferred_element_ty...]
    pallas_call x0 -> x17, Pallas kernels: none -> 463 us  [the longest x4 278 us: attn(): pl.pallas_call(attn_kernel, out_shape=(jax.ShapeDtypeStruct(x.shape, bf16...]
    all_to_all x0 -> x5, blocking collectives: none -> 258 us  [the longest x3 179 us: local_fn(): lax.all_to_all(split_heads(q, k, v, d_out, s, n_dev), 'cp', 0, 0)]
    dot_general x13 -> x0, matrix products: 207 us -> none  [the longest x2 36 us: block_scores(): jnp.einsum('qhd,shd->hqs', q_v, window, preferred_element_type=jnp.float32)]
    psum x1 -> x0, blocking collectives: 200 us -> none  [local_fn(): d_u_bias = lax.psum(grad_qu.sum(axis=0), 'cp')]
  transfers between devices with their start and end apart: 47 -> 8, of which waited for: 43 -> 1; matrix products, arithmetic and copies ran while one was open for 5% -> 4% of each run, Pallas kernels for 0% -> 37%
where the time goes in v1:
time: 982 us; the launch traced here: 969 us
  Pallas kernels  463 us (47%)
  blocking collectives  313 us (32%)
  waiting for transfers between devices  111 us (11%)
  local copies, waits for them, and re-layouts  56.2 us (6%)
  between operations  14.4 us (1%)
  starting transfers between devices  11.1 us (1%)
    pallas_call x4, Pallas kernels, attn(): pl.pallas_call(attn_kernel, out_shape=(jax.ShapeDtypeStruct(x.shape, bf16...  278 us
    all_to_all x3, blocking collectives, local_fn(): lax.all_to_all(split_heads(q, k, v, d_out, s, n_dev), 'cp', 0, 0)  179 us
    pallas_call x4, Pallas kernels, dw_matmul(): pl.pallas_call(dw_kernel, grid=(M // MB,), out_shape=jax.ShapeDtypeStruct...  136 us
    all_gather x1, waiting for transfers between devices, local_fn(): table = lax.all_gather(rel_table, 'cp', tiled=True)  111 us
    all_to_all x2, blocking collectives, local_fn(): z = lax.all_to_all(y, 'cp', 0, 0)  79 us
    all_gather x1, blocking collectives, local_fn(): sums = lax.all_gather(jnp.concatenate(sums, axis=1), 'cp')  55.1 us
    dynamic_slice x1, local copies, waits for them, and re-layouts, local_fn(): lax.dynamic_index_in_dim(w_rel.reshape(M, steps, n_dev, D), me, 2, keepdi...  29.3 us
    unnamed x43, local copies, waits for them, and re-layouts  20.7 us
  transfers between devices with their start and end apart: 8, of which 1 were waited for; matrix products, arithmetic and copies ran while one was open for 4% of the time, Pallas kernels for 37%

profile of v1, /device:TPU:0, one launch (start us, length us, event | category | flops | bytes accessed | tf_op | source)
XLA Modules:
  0.0 969.1 jit_solution(13661114829263033585)
XLA Ops:
  7.2 0.0 all-gather.11.cloned.1.call-start
  7.2 0.7 all-gather.11.cloned.1.call-update
  7.9 1.1 copy-done
  9.1 1.9 copy-done.1
  10.9 1.9 copy-done.5
  12.8 3.2 shard_map.142
  16.0 0.0 copy-start.10
  16.0 1.7 copy-done.10
  17.7 4.3 all-to-all-start.6
  22.0 0.0 all-gather.19.cloned.1.call-start
  22.0 29.3 %dynamic-slice_reduce_fusion = bf16[4096,4,128]{2,1,0:T(4,128)(2,1)S(1)} fusion(bf16[4096,4,8,128]{3,2,1,0:T(8,128)(2,1)} %bitcast.50, s32[]{:T(128)S(6)} %select_n.7), kind=kLoop, calls=%fused_computation | loop fusion | bytes 8388612 | tf_op jit(solution)/shard_map/jit(dynamic_index_in_dim)/dynamic_slice | solution.py:280
  51.3 2.7 copy.41
  54.1 1.4 fusion
  55.5 110.5 %all-gather.11.cloned.1.call-done.t_ref = bf16[3072,4096]{1,0:T(8,128)(2,1)} async-done(((bf16[384,4096]{1,0:T(8,128)(2,1)}), bf16[3072,4096]{1,0:T(8,128)(2,1)}) %all-gather.11.cloned.1.call-update) | async-done | bytes 25165840 | tf_op jit(solution)/shard_map/all_gather | solution.py:279
  166.0 19.1 %shard_map.136 = bf16[3072,512]{1,0:T(8,128)(2,1)} custom-call(bf16[3072,4096]{1,0:T(8,128)(2,1)} %all-gather.11.cloned.1.call-done.t_ref, bf16[4096,512]{1,0:T(8,128)(2,1)} %bitcast.49), custom_call_target="tpu_custom_call" | custom-call | flops 12884901888 | bytes 32505856 | tf_op jit(solution)/shard_map/pallas_call | solution.py:257
  185.1 3.6 fusion.8
  188.7 0.0 all-to-all-done.6.x_ref
  188.7 69.4 %shard_map.143 = (bf16[8,4,384,128]{3,2,1,0:T(8,128)(2,1)}, bf16[3072,128]{1,0:T(8,128)(2,1)}, f32[1,128]{1,0:T(1,128)}, f32[1,128]{1,0:T(1,128)}) custom-call(bf16[8,4,384,128]{3,2,1,0:T(8,128)(2,1)} %all-to-all-done.6.x_ref, bf16[3072,128]{1,0:T(8,128)(2,1)} %get-tuple-element.71.rel_ref, f32[1,128]{1,0:T(1,128)} %get-tuple-element.81.ub_ref, ...), custom_call_target="tpu_custom_call" | custom-call | flops 10871635968 | bytes 6291456 | tf_op jit(solution)/shard_map/pallas_call | solution.py:160
  258.1 0.0 all-gather.19.cloned.1.call-update
  258.1 0.2 all-gather.17.cloned.1.call-start
  258.4 0.0 copy-start.2
  258.4 1.9 copy-done.2
  260.3 1.9 copy-done.6
  262.1 3.2 shard_map.140
  265.3 60.3 %all_to_all.40.x_ref = bf16[8,4,384,128]{3,2,1,0:T(8,128)(2,1)} all-to-all(bf16[8,4,384,128]{3,2,1,0:T(8,128)(2,1)S(1)} %shard_map.140), channel_id=1, replica_groups=mesh['hp'=1,'cp'=8] {'cp'}, dimensions={0} | all-to-all | bytes 6291456 | tf_op jit(solution)/shard_map/all_to_all | solution.py:283
  325.6 69.4 %shard_map.141 = (bf16[8,4,384,128]{3,2,1,0:T(8,128)(2,1)}, bf16[3072,128]{1,0:T(8,128)(2,1)}, f32[1,128]{1,0:T(1,128)}, f32[1,128]{1,0:T(1,128)}) custom-call(bf16[8,4,384,128]{3,2,1,0:T(8,128)(2,1)} %all_to_all.40.x_ref, bf16[3072,128]{1,0:T(8,128)(2,1)} %get-tuple-element.72.rel_ref, f32[1,128]{1,0:T(1,128)} %get-tuple-element.82.ub_ref, ...), custom_call_target="tpu_custom_call" | custom-call | flops 10871635968 | bytes 6291456 | tf_op jit(solution)/shard_map/pallas_call | solution.py:160
  395.0 0.0 all-gather.17.cloned.1.call-update
  395.1 0.0 all-gather.15.cloned.1.call-start
  395.1 0.0 copy-start.3
  395.1 1.9 copy-done.3
  397.0 1.9 copy-done.7
  398.9 3.2 shard_map.138
  402.1 59.5 %all_to_all.41.x_ref = bf16[8,4,384,128]{3,2,1,0:T(8,128)(2,1)} all-to-all(bf16[8,4,384,128]{3,2,1,0:T(8,128)(2,1)S(1)} %shard_map.138), channel_id=1, replica_groups=mesh['hp'=1,'cp'=8] {'cp'}, dimensions={0} | all-to-all | bytes 6291456 | tf_op jit(solution)/shard_map/all_to_all | solution.py:283
  461.6 69.4 %shard_map.139 = (bf16[8,4,384,128]{3,2,1,0:T(8,128)(2,1)}, bf16[3072,128]{1,0:T(8,128)(2,1)}, f32[1,128]{1,0:T(1,128)}, f32[1,128]{1,0:T(1,128)}) custom-call(bf16[8,4,384,128]{3,2,1,0:T(8,128)(2,1)} %all_to_all.41.x_ref, bf16[3072,128]{1,0:T(8,128)(2,1)} %get-tuple-element.73.rel_ref, f32[1,128]{1,0:T(1,128)} %get-tuple-element.83.ub_ref, ...), custom_call_target="tpu_custom_call" | custom-call | flops 10871635968 | bytes 6291456 | tf_op jit(solution)/shard_map/pallas_call | solution.py:160
  531.0 0.0 all-gather.15.cloned.1.call-update
  531.1 0.0 copy-start.4
  531.1 1.9 copy-done.4
  532.9 1.9 copy-done.8
  534.8 3.2 shard_map.135
  538.0 0.0 copy-start.11
  538.0 59.6 %all_to_all.42.x_ref = bf16[8,4,384,128]{3,2,1,0:T(8,128)(2,1)} all-to-all(bf16[8,4,384,128]{3,2,1,0:T(8,128)(2,1)S(1)} %shard_map.135), channel_id=1, replica_groups=mesh['hp'=1,'cp'=8] {'cp'}, dimensions={0} | all-to-all | bytes 6291456 | tf_op jit(solution)/shard_map/all_to_all | solution.py:283
  597.6 39.3 %all_to_all.43.refs_0_ = bf16[8,4,384,128]{3,2,1,0:T(8,128)(2,1)S(1)} all-to-all(bf16[8,4,384,128]{3,2,1,0:T(8,128)(2,1)S(1)} %copy-done.11), channel_id=1, replica_groups=mesh['hp'=1,'cp'=8] {'cp'}, dimensions={0} | all-to-all | bytes 6291456 | tf_op jit(solution)/shard_map/all_to_all | solution.py:290
  636.9 39.7 %all_to_all.44.refs_0_ = bf16[8,4,384,128]{3,2,1,0:T(8,128)(2,1)} all-to-all(bf16[8,4,384,128]{3,2,1,0:T(8,128)(2,1)S(1)} %copy-done.12), channel_id=1, replica_groups=mesh['hp'=1,'cp'=8] {'cp'}, dimensions={0} | all-to-all | bytes 6291456 | tf_op jit(solution)/shard_map/all_to_all | solution.py:290
  676.6 3.2 all-to-all-start.3
  679.8 0.0 all-gather.13.cloned.1.call-start
  679.9 69.4 %shard_map.137 = (bf16[8,4,384,128]{3,2,1,0:T(8,128)(2,1)}, bf16[3072,128]{1,0:T(8,128)(2,1)}, f32[1,128]{1,0:T(1,128)}, f32[1,128]{1,0:T(1,128)}) custom-call(bf16[8,4,384,128]{3,2,1,0:T(8,128)(2,1)} %all_to_all.42.x_ref, bf16[3072,128]{1,0:T(8,128)(2,1)} %get-tuple-element.74.rel_ref, f32[1,128]{1,0:T(1,128)} %get-tuple-element.84.ub_ref, ...), custom_call_target="tpu_custom_call" | custom-call | flops 10871635968 | bytes 6291456 | tf_op jit(solution)/shard_map/pallas_call | solution.py:160
  749.3 0.0 all-gather.13.cloned.1.call-update
  749.3 0.0 all-to-all-done.3.refs_0_
  749.4 0.0 copy-start.17
  749.4 0.0 copy-start.19
  749.4 0.0 copy-start.20
  749.4 3.2 all-to-all-start.1
  752.7 55.1 %all-gather = f32[16,4,128]{2,1,0:T(4,128)S(1)} all-gather(f32[2,4,128]{2,1,0:T(4,128)S(1)} %maximum_maximum_fusion), channel_id=2, replica_groups=mesh['hp'=1,'cp'=8] {'cp'}, dimensions={0}, use_global_device_ids=true | all-gather | bytes 36864 | tf_op jit(solution)/shard_map/all_gather | solution.py:293
  807.8 0.6 copy.42
  808.4 0.6 copy.43
  809.0 3.4 shard_map.144
  812.4 3.4 shard_map.145
  815.8 5.0 shard_map.146
  820.8 0.0 all-to-all-done.1.refs_0_
  820.8 5.0 shard_map.147
  825.8 34.1 %shard_map.148.rest_0_ = f32[4096,32,128]{2,1,0:T(8,128)} custom-call(bf16[3072,4096]{1,0:T(8,128)(2,1)} %all-gather.11.cloned.1.call-done.t_ref, bf16[8,3072,128]{2,1,0:T(8,128)(2,1)} %bitcast.48), custom_call_target="tpu_custom_call" | custom-call | flops 25769803776 | bytes 48234496 | tf_op jit(solution)/shard_map/pallas_call | solution.py:237
  859.9 34.1 %shard_map.149.rest_0_ = f32[4096,32,128]{2,1,0:T(8,128)} custom-call(bf16[3072,4096]{1,0:T(8,128)(2,1)} %all-gather.11.cloned.1.call-done.t_ref, bf16[8,3072,128]{2,1,0:T(8,128)(2,1)} %bitcast.45, f32[4096,32,128]{2,1,0:T(8,128)} %shard_map.148.rest_0_), custom_call_target="tpu_custom_call", output_to_operand_aliasing={{}: (2, {})} | custom-call | flops 25769803776 | bytes 48234496 | tf_op jit(solution)/shard_map/pallas_call | solution.py:237
  894.0 34.1 %shard_map.150.rest_0_ = f32[4096,32,128]{2,1,0:T(8,128)} custom-call(bf16[3072,4096]{1,0:T(8,128)(2,1)} %all-gather.11.cloned.1.call-done.t_ref, bf16[8,3072,128]{2,1,0:T(8,128)(2,1)} %bitcast.46, f32[4096,32,128]{2,1,0:T(8,128)} %shard_map.149.rest_0_), custom_call_target="tpu_custom_call", output_to_operand_aliasing={{}: (2, {})} | custom-call | flops 25769803776 | bytes 48234496 | tf_op jit(solution)/shard_map/pallas_call | solution.py:237
  928.1 34.1 %shard_map.151 = f32[4096,32,128]{2,1,0:T(8,128)} custom-call(bf16[3072,4096]{1,0:T(8,128)(2,1)} %all-gather.11.cloned.1.call-done.t_ref, bf16[8,3072,128]{2,1,0:T(8,128)(2,1)} %bitcast.47, f32[4096,32,128]{2,1,0:T(8,128)} %shard_map.150.rest_0_), custom_call_target="tpu_custom_call", output_to_operand_aliasing={{}: (2, {})} | custom-call | flops 25769803776 | bytes 48234496 | tf_op jit(solution)/shard_map/pallas_call | solution.py:237
  (30 shorter events, 0.1 us)
Async XLA Ops:
  7.2 1.9 copy-start
  7.2 158.8 %all-gather.11.cloned.1.call-start = ((), (), s32[]{:S(2)}) async-start(), calls=%async_computation.8 | async-start | bytes 28311552 | tf_op jit(solution)/shard_map/all_gather | solution.py:279
  9.1 1.9 copy-start.1
  10.9 1.9 copy-start.5
  16.0 1.7 copy-start.10
  17.7 171.0 %all-to-all-start.6 = ((bf16[8,4,384,128]{3,2,1,0:T(8,128)(2,1)}), bf16[8,4,384,128]{3,2,1,0:T(8,128)(2,1)}, u32[]{:S(2)}, u32[]{:S(2)}) async-start(bf16[8,4,384,128]{3,2,1,0:T(8,128)(2,1)} %copy-done.10), calls=%async_computation.6 | async-start | bytes 6291456 | tf_op jit(solution)/shard_map/all_to_all | solution.py:283
  22.0 803.8 %all-gather.19.cloned.1.call-start = ((), (), s32[]{:S(2)}) async-start(), calls=%async_computation.12 | async-start | bytes 7077888 | tf_op jit(solution)/shard_map/all_gather | solution.py:289
  258.1 601.8 %all-gather.17.cloned.1.call-start = ((), (), s32[]{:S(2)}) async-start(), calls=%async_computation.11 | async-start | bytes 7077888 | tf_op jit(solution)/shard_map/all_gather | solution.py:289
  258.4 1.9 copy-start.2
  260.3 1.9 copy-start.6
  395.1 499.0 %all-gather.15.cloned.1.call-start = ((), (), s32[]{:S(2)}) async-start(), calls=%async_computation.10 | async-start | bytes 7077888 | tf_op jit(solution)/shard_map/all_gather | solution.py:289
  395.1 1.9 copy-start.3
  397.0 1.9 copy-start.7
  531.1 1.9 copy-start.4
  532.9 1.9 copy-start.8
  538.0 59.6 %copy-start.11 = (bf16[8,4,384,128]{3,2,1,0:T(8,128)(2,1)S(1)}, bf16[8,4,384,128]{3,2,1,0:T(8,128)(2,1)}, u32[]{:S(2)}) copy-start(bf16[8,4,384,128]{3,2,1,0:T(8,128)(2,1)} %get-tuple-element.42) | copy-start | bytes 9437188
  597.6 39.3 %copy-start.12 = (bf16[8,4,384,128]{3,2,1,0:T(8,128)(2,1)S(1)}, bf16[8,4,384,128]{3,2,1,0:T(8,128)(2,1)}, u32[]{:S(2)}) copy-start(bf16[8,4,384,128]{3,2,1,0:T(8,128)(2,1)} %get-tuple-element.41) | copy-start | bytes 9437188
  676.6 72.7 %all-to-all-start.3 = ((bf16[8,4,384,128]{3,2,1,0:T(8,128)(2,1)}), bf16[8,4,384,128]{3,2,1,0:T(8,128)(2,1)}, u32[]{:S(2)}, u32[]{:S(2)}) async-start(bf16[8,4,384,128]{3,2,1,0:T(8,128)(2,1)} %get-tuple-element.40), calls=%async_computation.3 | async-start | bytes 6291456 | tf_op jit(solution)/shard_map/all_to_all | solution.py:290
  679.8 248.3 %all-gather.13.cloned.1.call-start = ((), (), s32[]{:S(2)}) async-start(), calls=%async_computation.9 | async-start | bytes 7077888 | tf_op jit(solution)/shard_map/all_gather | solution.py:289
  749.3 3.3 copy-start.13
  749.4 3.3 copy-start.14
  749.4 3.3 copy-start.15
  749.4 3.3 copy-start.16
  749.4 3.3 copy-start.17
  749.4 3.3 copy-start.18
  749.4 3.3 copy-start.19
  749.4 3.3 copy-start.20
  749.4 71.4 %all-to-all-start.1 = ((bf16[8,4,384,128]{3,2,1,0:T(8,128)(2,1)}), bf16[8,4,384,128]{3,2,1,0:T(8,128)(2,1)}, u32[]{:S(2)}, u32[]{:S(2)}) async-start(bf16[8,4,384,128]{3,2,1,0:T(8,128)(2,1)} %get-tuple-element.39), calls=%async_computation.1 | async-start | bytes 6291456 | tf_op jit(solution)/shard_map/all_to_all | solution.py:290
  752.6 59.8 %copy-start.9 = (bf16[8,4,384,128]{3,2,1,0:T(8,128)(2,1)S(1)}, bf16[8,4,384,128]{3,2,1,0:T(8,128)(2,1)}, u32[]{:S(2)}) copy-start(bf16[8,4,384,128]{3,2,1,0:T(8,128)(2,1)} %all_to_all.44.refs_0_) | copy-start | bytes 9437188
Sparse Core Ops, SparseCore 0:
  9.8 156.1 all-gather.10
  258.3 67.8 all-gather.18
  395.2 66.9 all-gather.16
  531.2 66.9 all-gather.14
  749.5 68.0 all-gather.12
